TPU v7x, 32 devices: a whole 2x2x4 slice. The times are simulated.
32 devices in a mesh: up: 8 (over z, core), down: 4 (over y, x).
Axes of the slice: x: 2, y: 2, z: 4, core: 2. Of those that a mesh axis runs over, the one named last changes fastest.
Arguments:
- deltas: bfloat16 [256, 4096], P('down', 'up'), may hold values from -6 to 6
- gradients: bfloat16 [256, 4096], P('up', 'down'), may hold values from -0.375 to 0.375
- up_blocks: int32 [8, 16], P(None, 'up'), may hold values from 0 to 3, as said below
- down_blocks: int32 [16], P('down'), may hold values from 0 to 7, as said below
- decoder: bfloat16 [4096, 4608], P('up', 'down'), may hold values from -0.09375 to 0.09375
- encoder: bfloat16 [4608, 4096], P('up', 'down'), may hold values from -6 to 6
Outputs:
- edge_scores: float32 [4096, 4096], P('up', 'down')
Inputs may be any that keep to these rules, and one draw needn't show every extreme that they name: `up_blocks`: for each window and each index i of up, the 2 entries in columns i * 2 to (i + 1) * 2 - 1 are distinct. `down_blocks`: for each index j of down, the 4 entries j * 4 to (j + 1) * 4 - 1 are distinct.
All inputs are finite; a program needn't handle non-finite values.
Results may differ from a plain program's by a relative error of at most 0.0003.
Values may be sent and summed in bfloat16 or wider, within the bound.
A program may use at most 64 MiB of HBM per device.

v0:
```python
import jax
import jax.numpy as jnp
from jax import lax
from jax.sharding import PartitionSpec as P

UF_DEV = 512
VF_DEV = 1024
BLOCK = 128
DACT = 4
WIN = 32


def local(deltas, gradients, up_blocks, down_blocks, decoder, encoder):
    token_deltas = lax.all_gather(deltas, "down", axis=0, tiled=True)
    token_grads = lax.all_gather(gradients, "up", axis=0, tiled=True)
    tokens_all = token_deltas.shape[0]
    windows = tokens_all // WIN
    row_blocks = UF_DEV // BLOCK
    col_blocks = VF_DEV // BLOCK
    local_ids = jnp.arange(row_blocks, dtype=jnp.int32)
    block_on = jnp.any(up_blocks[:, :, None] == local_ids[None, None, :], axis=1)
    masked = token_deltas.reshape(windows, WIN, row_blocks, BLOCK) * block_on[
        :, None, :, None
    ].astype(token_deltas.dtype)
    masked = masked.reshape(tokens_all, UF_DEV)
    dec_whole = lax.all_gather(decoder, "down", axis=1, tiled=True)
    enc_height = encoder.shape[0]
    enc_used = jnp.take(
        encoder.reshape(enc_height, col_blocks, BLOCK), down_blocks, axis=1
    ).reshape(enc_height, DACT * BLOCK)
    virtual = jnp.dot(
        dec_whole,
        lax.all_gather(enc_used, "up", axis=0, tiled=True),
        preferred_element_type=jnp.float32,
    )
    grad_used = jnp.take(
        token_grads.reshape(tokens_all, col_blocks, BLOCK), down_blocks, axis=1
    ).reshape(tokens_all, DACT * BLOCK)
    product = lax.dot_general(
        masked, grad_used, (((0,), (0,)), ((), ())), preferred_element_type=jnp.float32
    )
    scored = (product * virtual).reshape(UF_DEV, DACT, BLOCK)
    filled = jnp.zeros((UF_DEV, col_blocks, BLOCK), jnp.float32).at[:, down_blocks, :].set(scored)
    return filled.reshape(UF_DEV, VF_DEV)


def solution(mesh):
    placed = (
        P("down", "up"),
        P("up", "down"),
        P(None, "up"),
        P("down"),
        P("up", "down"),
        P("up", "down"),
    )
    return jax.shard_map(
        local, mesh=mesh, in_specs=placed, out_specs=P("up", "down"), check_vma=False
    )
```

profile of v0, /device:TPU:1, one launch (start us, length us, event | category | flops | bytes accessed | tf_op | source)
XLA Modules:
  0.0 143.8 jit_solution(9845222064683501501)
XLA Ops:
  6.5 0.0 copy-start
  6.5 0.0 all-gather.5.cloned.1.call-start
  6.5 0.7 all-gather.5.cloned.1.call-update
  7.3 0.0 all-gather.3.cloned.1.call-start
  7.3 0.7 compare_select_fusion
  8.0 0.0 copy-done
  8.0 0.0 copy-start.1
  8.0 0.2 copy_bitcast_fusion
  8.2 0.7 gather_fusion.1
  8.9 0.0 copy-done.4
  8.9 0.1 broadcast_bitcast_fusion
  9.0 0.9 bitcast_select_fusion
  9.9 0.0 all-gather.3.cloned.1.call-update
  9.9 0.0 copy-done.1
  9.9 16.4 %all_gather.13 = bf16[256,1024]{1,0:T(8,128)(2,1)S(1)} all-gather(bf16[32,1024]{1,0:T(8,128)(2,1)S(1)} %copy-done.1), channel_id=1, replica_groups=mesh['up'=8,'down'=4] {'up'}, dimensions={0}, use_global_device_ids=true | all-gather | bytes 589824 | tf_op jit(solution)/shard_map/all_gather | solution.py:15
  26.3 0.2 copy.32
  26.5 0.3 copy.33
  26.8 0.6 gather_fusion
  27.4 0.1 copy.34
  27.6 0.1 copy.31
  27.7 9.2 %all_gather.12 = bf16[256,512]{1,0:T(8,128)(2,1)S(1)} all-gather(bf16[64,512]{1,0:T(8,128)(2,1)S(1)} %copy-done.2), channel_id=1, replica_groups=mesh['up'=8,'down'=4] {'down'}, dimensions={0}, use_global_device_ids=true | all-gather | bytes 327680 | tf_op jit(solution)/shard_map/all_gather | solution.py:14
  36.9 0.1 bitcast_select_fusion.1
  37.1 0.1 mul.14
  37.2 0.3 fusion.1
  37.5 31.7 %all-gather.5.cloned.1.call-done = bf16[512,4608]{1,0:T(8,128)(2,1)} async-done(((bf16[512,1152]{1,0:T(8,128)(2,1)}), bf16[512,4608]{1,0:T(8,128)(2,1)}) %all-gather.5.cloned.1.call-update) | async-done | bytes 4718608 | tf_op jit(solution)/shard_map/all_gather | solution.py:26
  69.2 53.4 %all-gather.3.cloned.1.call-done = bf16[4608,512]{1,0:T(8,128)(2,1)} async-done(((bf16[576,512]{1,0:T(8,128)(2,1)}), bf16[4608,512]{1,0:T(8,128)(2,1)}) %all-gather.3.cloned.1.call-update) | async-done | bytes 4718608 | tf_op jit(solution)/shard_map/all_gather | solution.py:33
  122.7 6.1 %fusion = f32[512,512]{0,1:T(8,128)S(1)} fusion(f32[512,512]{0,1:T(8,128)S(1)} %fusion.1, bf16[4608,512]{1,0:T(8,128)(2,1)} %all-gather.3.cloned.1.call-done, bf16[512,4608]{1,0:T(8,128)(2,1)} %all-gather.5.cloned.1.call-done), kind=kOutput, calls=%fused_computation.4 | convolution fusion | flops 2416181248 | bytes 11534336 | tf_op jit(solution)/shard_map/dot_general | solution.py:31
  128.8 1.3 copy.37
  130.1 0.1 broadcast_in_dim.33
  130.2 1.9 %scatter_fusion = f32[512,8,128]{2,0,1:T(8,128)S(1)} fusion(f32[512,8,128]{2,0,1:T(8,128)S(1)} %broadcast_in_dim.33, s32[4]{0:T(128)S(1)} %compare_select_fusion, f32[4,512,128]{2,1,0:T(8,128)} %bitcast.33), kind=kCustom, calls=%fused_computation.2 | custom fusion | bytes 3145744 | tf_op jit(solution)/shard_map/scatter | solution.py:43
  132.2 1.9 %copy.38 = f32[512,8,128]{0,2,1:T(8,128)} copy(f32[512,8,128]{2,0,1:T(8,128)S(1)} %scatter_fusion) | data formatting | bytes 4194304 | tf_op jit(solution)/shard_map/scatter | solution.py:43
  134.1 2.9 %copy.39 = f32[512,1024]{1,0:T(8,128)} copy(f32[512,1024]{0,1:T(8,128)} %bitcast.32) | data formatting | bytes 4194304 | tf_op jit(solution)/shard_map/reshape | solution.py:44
  (9 shorter events, 0.0 us)
Async XLA Ops:
  6.5 1.4 %copy-start = (bf16[576,1024]{1,0:T(8,128)(2,1)S(1)}, bf16[576,1024]{1,0:T(8,128)(2,1)}, u32[]{:S(2)}) copy-start(bf16[576,1024]{1,0:T(8,128)(2,1)} %param.11) | copy-start | bytes 3538948
  6.5 2.3 %copy-start.4 = (s32[4]{0:T(128)S(1)}, s32[4]{0:T(128)}, u32[]{:S(2)}) copy-start(s32[4]{0:T(128)} %param.9) | copy-start | bytes 52
  6.5 62.7 %all-gather.5.cloned.1.call-start = ((), (), s32[]{:S(2)}) async-start(), calls=%async_computation.1 | async-start | bytes 5898240 | tf_op jit(solution)/shard_map/all_gather | solution.py:26
  7.3 115.4 %all-gather.3.cloned.1.call-start = ((), (), s32[]{:S(2)}) async-start(), calls=%async_computation | async-start | bytes 5308416 | tf_op jit(solution)/shard_map/all_gather | solution.py:33
  8.0 2.0 %copy-start.1 = (bf16[32,1024]{1,0:T(8,128)(2,1)S(1)}, bf16[32,1024]{1,0:T(8,128)(2,1)}, u32[]{:S(2)}) copy-start(bf16[32,1024]{1,0:T(8,128)(2,1)} %param.7) | copy-start | bytes 196612
  9.9 17.6 %copy-start.3 = (s32[8,2]{0,1:T(2,128)S(1)}, s32[8,2]{0,1:T(2,128)}, u32[]{:S(2)}) copy-start(s32[8,2]{0,1:T(2,128)} %param.8) | copy-start | bytes 196
  9.9 17.8 %copy-start.2 = (bf16[64,512]{1,0:T(8,128)(2,1)S(1)}, bf16[64,512]{1,0:T(8,128)(2,1)}, u32[]{:S(2)}) copy-start(bf16[64,512]{1,0:T(8,128)(2,1)} %param.6) | copy-start | bytes 196612
Sparse Core Ops, SparseCore 0:
  9.2 60.0 all-gather.4
  70.9 51.7 all-gather.2
where the time goes:
time: 144 us
  waiting for transfers between devices  85.9 us (60%)
  blocking collectives  25.6 us (18%)
  between operations  13.5 us (9%)
  local copies, waits for them, and re-layouts  10.6 us (7%)
  matrix products  6.41 us (4%)
  other arithmetic  1.76 us (1%)
    all_gather x1, waiting for transfers between devices, local(): lax.all_gather(enc_used, 'up', axis=0, tiled=True)  53.4 us
    all_gather x1, waiting for transfers between devices, local(): dec_whole = lax.all_gather(decoder, 'down', axis=1, tiled=True)  31.7 us
    all_gather x1, blocking collectives, local(): token_grads = lax.all_gather(gradients, 'up', axis=0, tiled=True)  16.4 us
    all_gather x1, blocking collectives, local(): token_deltas = lax.all_gather(deltas, 'down', axis=0, tiled=True)  9.23 us
    dot_general x1, matrix products, local(): jnp.dot(dec_whole, lax.all_gather(enc_used, 'up', axis=0, tiled=True), pr...  6.1 us
    scatter x2, local copies, waits for them, and re-layouts, local(): jnp.zeros((UF_DEV, col_blocks, BLOCK), jnp.float32).at[:, down_blocks, :]  3.82 us
  transfers between devices with their start and end apart: 2, of which 2 were waited for; matrix products, arithmetic and copies ran while one was open for 3% of the time, Pallas kernels for 0%

commit v1 on v0

v1 whole, which is shorter than its diff:
```python
import functools

import jax
import jax.numpy as jnp
from jax import lax
from jax.experimental import pallas as pl
from jax.experimental.pallas import tpu as pltpu
from jax.sharding import PartitionSpec as P

BLOCK = 128
MESH = pl.DeviceIdType.MESH
F32 = jnp.float32


def flag(number, block, kind):
    return jnp.where(jnp.full((1, BLOCK), number, jnp.int32) == block, 1.0, 0.0).astype(kind)


def pick(ref, rows, number, blocks):
    total = None
    for b in range(blocks):
        term = ref[rows, b * BLOCK:(b + 1) * BLOCK] * flag(number, b, ref.dtype)
        total = term if total is None else total + term
    return total


def gather_scores(
    n_up, n_down, upb, downb, deltas, grads, dec, enc, out,
    dec_all, enc_raw, enc_all, del_raw, del_all, grad_raw, grad_all, masked, acc, prod,
    load_sem, dec_send, dec_recv, del_send, del_recv, enc_send, enc_recv,
    grad_send, grad_recv, pair_send, pair_recv, pg_send, pg_recv,
):
    levels = n_up // 2
    rows, depth = dec.shape
    height = enc.shape[0]
    half = height // 2
    chunk = rows // 4
    toks = grads.shape[0]
    wins = del_all.shape[1]
    win = del_all.shape[2]
    uact = upb.shape[1]
    dact = downb.shape[0]
    up, down = lax.axis_index("up"), lax.axis_index("down")
    z, core = up // 2, up % 2
    place = lambda d: 2 * (d // 2) + (d + d // 2) % 2
    pos = place(down)
    right, left = place((pos + 1) % 4), place((pos + 3) % 4)
    diag = place((pos + 2) % 4)
    ring_to = ((up, right), (up, left))
    ring_from = (left, right)
    step_of = (1, -1)

    loads = [
        pltpu.make_async_copy(dec, dec_all.at[down], load_sem.at[0]),
        pltpu.make_async_copy(enc, enc_raw, load_sem.at[1]),
        pltpu.make_async_copy(deltas, del_raw, load_sem.at[2]),
        pltpu.make_async_copy(grads, grad_raw, load_sem.at[3]),
    ]
    for copy in loads:
        copy.start()

    barrier = pltpu.get_barrier_semaphore()
    can_go = (z < levels - 1, z > 0)
    for dev in (*ring_to, (2 * z + 1 - core, down)):
        pl.semaphore_signal(barrier, inc=1, device_id=dev, device_id_type=MESH)
    for r in range(2):
        @pl.when(can_go[r])
        def _():
            pl.semaphore_signal(barrier, inc=1, device_id=(up + 2 * step_of[r], down), device_id_type=MESH)

    loads[2].wait()
    for w in range(wins):
        for s in range(uact):
            del_all[down, w, :, s * BLOCK:(s + 1) * BLOCK] = pick(
                del_raw, slice(w * win, (w + 1) * win), upb[down * wins + w, s], rows // BLOCK)
    loads[3].wait()
    loads[1].wait()
    for s in range(dact):
        grad_all[pl.ds(pl.multiple_of(up * toks, toks), toks), s * BLOCK:(s + 1) * BLOCK] = pick(
            grad_raw, slice(0, toks), downb[s], enc.shape[1] // BLOCK)
        enc_all[pl.ds(pl.multiple_of(up * height, 16), height), s * BLOCK:(s + 1) * BLOCK] = pick(
            enc_raw, slice(0, height), downb[s], enc.shape[1] // BLOCK)
    loads[0].wait()
    expected = 3 + jnp.where(z < levels - 1, 1, 0) + jnp.where(z > 0, 1, 0)
    pl.semaphore_wait(barrier, expected)

    orders = ((0, 1, 2, 3), (2, 3, 0, 1))

    def dec_copy(r, i, owner):
        piece = orders[r][i % 4]
        ref = dec_all.at[owner, pl.ds(piece * chunk, chunk)]
        return pltpu.make_async_remote_copy(
            ref, ref, dec_send.at[r, i], dec_recv.at[r, i], device_id=ring_to[r], device_id_type=MESH)

    def del_copy(r, i, owner):
        piece = (i + r) % 2
        ref = del_all.at[owner, piece]
        return pltpu.make_async_remote_copy(
            ref, ref, del_send.at[r, i], del_recv.at[r, i], device_id=ring_to[r], device_id_type=MESH)

    def enc_rows(level, h, c):
        return enc_all.at[pl.ds(pl.multiple_of((level * 2 + c) * height + h * half, 16), half)]

    def enc_copy(r, k, level):
        ref = enc_rows(level, (k - 1) % 2, core)
        return pltpu.make_async_remote_copy(
            ref, ref, enc_send.at[r, k - 1], enc_recv.at[r, k - 1],
            device_id=(up + 2 * step_of[r], down), device_id_type=MESH)

    def grad_rows(level, c):
        return grad_all.at[pl.ds(pl.multiple_of((level * 2 + c) * toks, toks), toks)]

    def grad_copy(r, j, level):
        ref = grad_rows(level, core)
        return pltpu.make_async_remote_copy(
            ref, ref, grad_send.at[r, j - 1], grad_recv.at[r, j - 1],
            device_id=(up + 2 * step_of[r], down), device_id_type=MESH)

    def pair_copy(level, h, c):
        ref = enc_rows(level, h, c)
        return pltpu.make_async_remote_copy(
            ref, ref, pair_send.at[level, h], pair_recv.at[level, h],
            device_id=(2 * z + 1 - core, down), device_id_type=MESH)

    def pair_grad(level, c):
        ref = grad_rows(level, c)
        return pltpu.make_async_remote_copy(
            ref, ref, pg_send.at[level], pg_recv.at[level],
            device_id=(2 * z + 1 - core, down), device_id_type=MESH)

    inside = lambda level: jnp.logical_and(level >= 0, level < levels)

    for r in range(2):
        del_copy(r, 0, down).start()
        del_copy(r, 1, down).start()

        @pl.when(can_go[r])
        def _():
            grad_copy(r, 1, z).start()
    for i in range(2):
        for r in range(2):
            dec_copy(r, i, down).start()

            @pl.when(can_go[r])
            def _():
                enc_copy(r, i + 1, z).start()
    for i in range(2, 4):
        for r in range(2):
            dec_copy(r, i, down).start()
    pair_grad(z, core).start()
    for h in range(2):
        pair_copy(z, h, core).start()

    def quarter(q):
        for m in range(2):
            for n in range(2):
                rs, cs = slice(m * rows // 2, (m + 1) * rows // 2), slice(n * acc.shape[1] // 2, (n + 1) * acc.shape[1] // 2)
                acc[rs, cs] += jnp.dot(
                    dec_all[q, rs, :], enc_all[pl.ds(pl.multiple_of(q * depth, 128), depth), cs],
                    preferred_element_type=F32)

    far = lambda q: jnp.maximum(q - z, z - q) >= levels - 1
    late = [jnp.where(jnp.logical_or(diag == q, far(q)), 1, 0) for q in range(levels)]
    early = sum(1 - x for x in late)
    rank = []
    for q in range(levels):
        before = sum(late[:q]) if q else 0
        rank.append(jnp.where(late[q] == 1, early + before, q - before))
    order = [sum(jnp.where(rank[q] == s, q, 0) for q in range(levels)) for s in range(levels)]

    acc[...] = jnp.zeros_like(acc)

    for k in range(1, 2 * (levels - 1) + 1):
        j, h = (k + 1) // 2, (k - 1) % 2
        for r in range(2):
            if k == 1:
                del_copy(r, 0, ring_from[r]).wait_recv()
                del_copy(r, 2, ring_from[r]).start()
            if k <= 2:
                dec_copy(r, k - 1, ring_from[r]).wait_recv()
                dec_copy(r, k + 3, ring_from[r]).start()
        for r in range(2):
            level = z - step_of[r] * j

            @pl.when(inside(level))
            def _():
                if h == 0:
                    grad_copy(r, j, level).wait_recv()
                    if j < levels - 1:
                        @pl.when(can_go[r])
                        def _():
                            grad_copy(r, j + 1, level).start()
                    pair_grad(level, core).start()
                enc_copy(r, k, level).wait_recv()
                if j < levels - 1:
                    @pl.when(can_go[r])
                    def _():
                        enc_copy(r, k + 2, level).start()
                pair_copy(level, h, core).start()
        if k == 2 * (levels - 2):
            for r in range(2):
                for i in range(2, 4):
                    dec_copy(r, i, ring_from[r]).wait_recv()
            for lv in range(levels):
                @pl.when(jnp.logical_not(far(lv)))
                def _():
                    for h2 in range(2):
                        pair_copy(lv, h2, 1 - core).wait_recv()

            @pl.loop(0, 2)
            def _(s):
                quarter(jnp.where(s == 0, order[0], order[1]))
        if k == 2 * (levels - 2) + 1:
            for r in range(2):
                del_copy(r, 1, ring_from[r]).wait_recv()
                del_copy(r, 2, diag).wait_recv()
            for lv in range(levels):
                pair_grad(lv, 1 - core).wait_recv()
            for d in range(n_down):
                for w in range(wins):
                    for b in range(rows // BLOCK):
                        value = jnp.zeros((win, BLOCK), masked.dtype)
                        for s in range(uact):
                            on = flag(upb[d * wins + w, s], b, masked.dtype)
                            value = value + del_all[d, w, :, s * BLOCK:(s + 1) * BLOCK] * on
                        t = (d * wins + w) * win
                        masked[t:t + win, b * BLOCK:(b + 1) * BLOCK] = value
            prod[...] = lax.dot_general(
                masked[...], grad_all[...], (((0,), (0,)), ((), ())), preferred_element_type=F32)

    for r in range(2):
        for i in range(4, 6):
            dec_copy(r, i, diag).wait_recv()
    for lv in range(levels):
        @pl.when(far(lv))
        def _():
            for h2 in range(2):
                pair_copy(lv, h2, 1 - core).wait_recv()

    @pl.loop(2, 4)
    def _(s):
        quarter(jnp.where(s == 2, order[2], order[3]))
    out[...] = acc[...] * prod[...]

    for r in range(2):
        for i in range(3):
            del_copy(r, i, down).wait_send()
        for i in range(6):
            dec_copy(r, i, down).wait_send()
        for k in range(1, 2 * (levels - 1) + 1):
            @pl.when(jnp.logical_and(can_go[r], inside(z - step_of[r] * ((k - 1) // 2))))
            def _():
                enc_copy(r, k, z).wait_send()
                if k % 2:
                    grad_copy(r, (k + 1) // 2, z).wait_send()
    for lv in range(levels):
        pair_grad(lv, core).wait_send()
        for h in range(2):
            pair_copy(lv, h, core).wait_send()


def spread(downb, scored, out):
    for c in range(out.shape[1] // BLOCK):
        slot, on = 0, 0
        for s in range(downb.shape[0]):
            hit = (downb[s] == c).astype(jnp.int32)
            slot, on = slot + s * hit, on + hit
        value = scored[:, pl.ds(pl.multiple_of(slot * BLOCK, BLOCK), BLOCK)]
        out[:, c * BLOCK:(c + 1) * BLOCK] = jnp.where(on > 0, value, 0.0)


def ring_local(n_up, n_down, win, deltas, gradients, up_blocks, down_blocks, decoder, encoder):
    rows, depth = decoder.shape
    height, cols = encoder.shape
    toks = gradients.shape[0]
    uact, dact = up_blocks.shape[1], down_blocks.shape[0]
    tokens = deltas.shape[0] * n_down
    wins = deltas.shape[0] // win
    used = dact * BLOCK
    levels = n_up // 2
    kind = decoder.dtype
    dma = pltpu.SemaphoreType.DMA
    smem, anywhere = pl.BlockSpec(memory_space=pltpu.SMEM), pl.BlockSpec(memory_space=pl.ANY)
    vmem = pl.BlockSpec(memory_space=pltpu.VMEM)
    hops = 2 * (levels - 1)
    scored = pl.pallas_call(
        functools.partial(gather_scores, n_up, n_down),
        out_shape=jax.ShapeDtypeStruct((rows, used), F32),
        in_specs=[smem, smem, anywhere, anywhere, anywhere, anywhere],
        out_specs=vmem,
        scratch_shapes=[
            pltpu.VMEM((n_down, rows, depth), kind),
            pltpu.VMEM((height, cols), kind),
            pltpu.VMEM((n_up * height, used), kind),
            pltpu.VMEM(deltas.shape, kind),
            pltpu.VMEM((n_down, wins, win, uact * BLOCK), kind),
            pltpu.VMEM((toks, cols), kind),
            pltpu.VMEM((n_up * toks, used), kind),
            pltpu.VMEM((tokens, rows), kind),
            pltpu.VMEM((rows, used), F32),
            pltpu.VMEM((rows, used), F32),
            dma((4,)),
            dma((2, 6)), dma((2, 6)),
            dma((2, 3)), dma((2, 3)),
            dma((2, hops)), dma((2, hops)),
            dma((2, levels - 1)), dma((2, levels - 1)),
            dma((levels, 2)), dma((levels, 2)),
            dma((levels,)), dma((levels,)),
        ],
        compiler_params=pltpu.CompilerParams(collective_id=0, has_side_effects=True),
        name="gather_scores",
    )(up_blocks, down_blocks, deltas, gradients, decoder, encoder)
    tile = rows // 4
    return pl.pallas_call(
        spread,
        grid=(rows // tile,),
        out_shape=jax.ShapeDtypeStruct((rows, cols), F32),
        in_specs=[smem, pl.BlockSpec((tile, used), lambda i: (i, 0))],
        out_specs=pl.BlockSpec((tile, cols), lambda i: (i, 0)),
        name="spread",
    )(down_blocks, scored)


def plain_local(deltas, gradients, up_blocks, down_blocks, decoder, encoder):
    token_deltas = lax.all_gather(deltas, "down", axis=0, tiled=True)
    token_grads = lax.all_gather(gradients, "up", axis=0, tiled=True)
    tokens, rows = token_deltas.shape
    windows, dact = up_blocks.shape[0], down_blocks.shape[0]
    row_blocks, col_blocks = rows // BLOCK, encoder.shape[1] // BLOCK
    local_ids = jnp.arange(row_blocks, dtype=jnp.int32)
    block_on = jnp.any(up_blocks[:, :, None] == local_ids[None, None, :], axis=1)
    masked = token_deltas.reshape(windows, tokens // windows, row_blocks, BLOCK) * block_on[
        :, None, :, None].astype(token_deltas.dtype)
    masked = masked.reshape(tokens, rows)
    dec_whole = lax.all_gather(decoder, "down", axis=1, tiled=True)
    height = encoder.shape[0]
    enc_used = jnp.take(encoder.reshape(height, col_blocks, BLOCK), down_blocks, axis=1).reshape(height, dact * BLOCK)
    virtual = jnp.dot(dec_whole, lax.all_gather(enc_used, "up", axis=0, tiled=True), preferred_element_type=F32)
    grad_used = jnp.take(token_grads.reshape(tokens, col_blocks, BLOCK), down_blocks, axis=1).reshape(tokens, dact * BLOCK)
    product = lax.dot_general(masked, grad_used, (((0,), (0,)), ((), ())), preferred_element_type=F32)
    scored = (product * virtual).reshape(rows, dact, BLOCK)
    filled = jnp.zeros((rows, col_blocks, BLOCK), F32).at[:, down_blocks, :].set(scored)
    return filled.reshape(rows, encoder.shape[1])


def solution(mesh):
    n_up, n_down = mesh.shape["up"], mesh.shape["down"]
    ringed = n_down == 4 and n_up == 2 * n_down

    def local(deltas, gradients, up_blocks, down_blocks, decoder, encoder):
        args = (deltas, gradients, up_blocks, down_blocks, decoder, encoder)
        tokens = deltas.shape[0] * n_down
        win = tokens // up_blocks.shape[0]
        if ringed and deltas.shape[0] == 2 * win:
            return ring_local(n_up, n_down, win, *args)
        return plain_local(*args)

    placed = (P("down", "up"), P("up", "down"), P(None, "up"), P("down"), P("up", "down"), P("up", "down"))
    return jax.shard_map(local, mesh=mesh, in_specs=placed, out_specs=P("up", "down"), check_vma=False)
```

time: 144 us -> 56.9 us (0.40)
  waiting for transfers between devices: 85.9 us -> 0 us
  Pallas kernels: 0 us -> 55.3 us
  blocking collectives: 25.6 us -> 0 us
  between operations: 13.5 us -> 0.01 us
  local copies, waits for them, and re-layouts: 10.6 us -> 1.34 us
  matrix products: 6.41 us -> 0 us
  other arithmetic: 1.76 us -> 0 us
    all_gather x2 -> x0, waiting for transfers between devices: 85.2 us -> none  [the longest x1 53.4 us: local(): lax.all_gather(enc_used, 'up', axis=0, tiled=True)]
    pallas_call x0 -> x2, Pallas kernels: none -> 55.3 us  [the longest x1 51.6 us: ring_local(): pl.pallas_call(functools.partial(gather_scores, n_up, n_down), out_shape=...]
    all_gather x2 -> x0, blocking collectives: 25.6 us -> none  [the longest x1 16.4 us: local(): token_grads = lax.all_gather(gradients, 'up', axis=0, tiled=True)]
    dot_general x2 -> x0, matrix products: 6.41 us -> none  [the longest x1 6.1 us: local(): jnp.dot(dec_whole, lax.all_gather(enc_used, 'up', axis=0, tiled=True), pr...]
    reshape x4 -> x0, local copies, waits for them, and re-layouts: 4.67 us -> none  [the longest x1 2.88 us: local(): return filled.reshape(UF_DEV, VF_DEV)]
    scatter x2 -> x0, local copies, waits for them, and re-layouts: 3.82 us -> none  [local(): jnp.zeros((UF_DEV, col_blocks, BLOCK), jnp.float32).at[:, down_blocks, :]]
    select_n x3 -> x0, other arithmetic: 1.72 us -> none  [the longest x1 0.92 us: local(): jnp.take(encoder.reshape(enc_height, col_blocks, BLOCK), down_blocks, axi...]
  transfers between devices with their start and end apart: 2 -> 0, of which waited for: 2 -> 0; matrix products, arithmetic and copies ran while one was open for 3% -> 0% of each run, Pallas kernels for 0% -> 0%
where the time goes in v1:
time: 56.9 us; the launch traced here: 56.7 us
  Pallas kernels  55.3 us (97%)
  local copies, waits for them, and re-layouts  1.34 us (2%)
    pallas_call x1, Pallas kernels, ring_local(): pl.pallas_call(functools.partial(gather_scores, n_up, n_down), out_shape=...  51.6 us
    pallas_call x1, Pallas kernels, ring_local(): pl.pallas_call(spread, grid=(rows // tile,), out_shape=jax.ShapeDtypeStru...  3.71 us
    unnamed x1, local copies, waits for them, and re-layouts  1.34 us

profile of v1, /device:TPU:1, one launch (start us, length us, event | category | flops | bytes accessed | tf_op | source)
XLA Modules:
  0.0 56.7 jit_solution(6470626258028022107)
XLA Ops:
  0.0 1.3 %copy.7.upb = s32[8,2]{1,0:T(8,128)} copy(s32[8,2]{0,1:T(2,128)} %param.8) | data formatting | bytes 128 | tf_op args[2]
  1.3 51.6 %gather_scores.1.scored = f32[512,512]{1,0:T(8,128)} custom-call(s32[8,2]{1,0:T(8,128)} %copy.7.upb, s32[4]{0:T(128)} %downb.3, bf16[64,512]{1,0:T(8,128)(2,1)} %deltas.1, bf16[32,1024]{1,0:T(8,128)(2,1)} %grads.1, bf16[512,1152]{1,0:T(8,128)(2,1)} %dec.1, bf16[576,1024]{1,0:T(8,128)(2,1)} %enc.1), custom_call_target="tpu_custom_call" | custom-call | tf_op jit(solution)/shard_map/gather_scores/pallas_call | solution.py:286
  53.0 3.7 %spread.1 = f32[512,1024]{1,0:T(8,128)} custom-call(s32[4]{0:T(128)} %downb.3, f32[512,512]{1,0:T(8,128)} %gather_scores.1.scored), custom_call_target="tpu_custom_call" | custom-call | tf_op jit(solution)/shard_map/spread/pallas_call | solution.py:314

commit v2 on v1

--- a/solution.py
+++ b/solution.py
@@ -8,6 +8,7 @@
 from jax.sharding import PartitionSpec as P
 
 BLOCK = 128
+LARGE, SMALL = 24 << 20, 4 << 20
 MESH = pl.DeviceIdType.MESH
 F32 = jnp.float32
 
@@ -26,19 +27,19 @@
 
 def gather_scores(
     n_up, n_down, upb, downb, deltas, grads, dec, enc, out,
-    dec_all, enc_raw, enc_all, del_raw, del_all, grad_raw, grad_all, masked, acc, prod,
+    dec_all, enc_raw, enc_all, del_raw, del_all, grad_raw, grad_all, masked, acc, prod, res,
     load_sem, dec_send, dec_recv, del_send, del_recv, enc_send, enc_recv,
-    grad_send, grad_recv, pair_send, pair_recv, pg_send, pg_recv,
+    grad_send, grad_recv, pair_send, pair_recv, pg_send, pg_recv, out_sem,
 ):
     levels = n_up // 2
     rows, depth = dec.shape
     height = enc.shape[0]
-    half = height // 2
+    half = enc_all.shape[2]
     chunk = rows // 4
     toks = grads.shape[0]
     wins = del_all.shape[1]
     win = del_all.shape[2]
-    uact = upb.shape[1]
+    uact = upb.shape[0]
     dact = downb.shape[0]
     up, down = lax.axis_index("up"), lax.axis_index("down")
     z, core = up // 2, up % 2
@@ -72,19 +73,20 @@
     for w in range(wins):
         for s in range(uact):
             del_all[down, w, :, s * BLOCK:(s + 1) * BLOCK] = pick(
-                del_raw, slice(w * win, (w + 1) * win), upb[down * wins + w, s], rows // BLOCK)
+                del_raw, slice(w * win, (w + 1) * win), upb[s, down * wins + w], rows // BLOCK)
     loads[3].wait()
     loads[1].wait()
     for s in range(dact):
         grad_all[pl.ds(pl.multiple_of(up * toks, toks), toks), s * BLOCK:(s + 1) * BLOCK] = pick(
             grad_raw, slice(0, toks), downb[s], enc.shape[1] // BLOCK)
-        enc_all[pl.ds(pl.multiple_of(up * height, 16), height), s * BLOCK:(s + 1) * BLOCK] = pick(
+        side, at = divmod(s * BLOCK, half)
+        enc_all[side, pl.ds(pl.multiple_of(up * height, 16), height), at:at + BLOCK] = pick(
             enc_raw, slice(0, height), downb[s], enc.shape[1] // BLOCK)
     loads[0].wait()
     expected = 3 + jnp.where(z < levels - 1, 1, 0) + jnp.where(z > 0, 1, 0)
     pl.semaphore_wait(barrier, expected)
 
-    orders = ((0, 1, 2, 3), (2, 3, 0, 1))
+    orders = ((0, 2, 1, 3), (1, 3, 0, 2))
 
     def dec_copy(r, i, owner):
         piece = orders[r][i % 4]
@@ -99,7 +101,7 @@
             ref, ref, del_send.at[r, i], del_recv.at[r, i], device_id=ring_to[r], device_id_type=MESH)
 
     def enc_rows(level, h, c):
-        return enc_all.at[pl.ds(pl.multiple_of((level * 2 + c) * height + h * half, 16), half)]
+        return enc_all.at[h, pl.ds(pl.multiple_of((level * 2 + c) * height, 16), height)]
 
     def enc_copy(r, k, level):
         ref = enc_rows(level, (k - 1) % 2, core)
@@ -151,22 +153,34 @@
     for h in range(2):
         pair_copy(z, h, core).start()
 
-    def quarter(q):
-        for m in range(2):
-            for n in range(2):
-                rs, cs = slice(m * rows // 2, (m + 1) * rows // 2), slice(n * acc.shape[1] // 2, (n + 1) * acc.shape[1] // 2)
-                acc[rs, cs] += jnp.dot(
-                    dec_all[q, rs, :], enc_all[pl.ds(pl.multiple_of(q * depth, 128), depth), cs],
-                    preferred_element_type=F32)
-
-    far = lambda q: jnp.maximum(q - z, z - q) >= levels - 1
-    late = [jnp.where(jnp.logical_or(diag == q, far(q)), 1, 0) for q in range(levels)]
-    early = sum(1 - x for x in late)
-    rank = []
-    for q in range(levels):
-        before = sum(late[:q]) if q else 0
-        rank.append(jnp.where(late[q] == 1, early + before, q - before))
-    order = [sum(jnp.where(rank[q] == s, q, 0) for q in range(levels)) for s in range(levels)]
+    part = rows // 2
+
+    def product_unit(u, low, high):
+        q, m, n = u // 4, u // 2 % 2, u % 2
+        gap = jnp.maximum(q - z, z - q)
+        enc_hop = jnp.where(gap == 0, 0, 2 * gap - 1 + n)
+        dec_hop = jnp.where(q == diag, 5 + m, 4)
+        hop = jnp.maximum(enc_hop, dec_hop)
+
+        @pl.when(jnp.logical_and(hop >= low, hop <= high))
+        def _():
+            rs = pl.ds(pl.multiple_of(m * part, part), part)
+            acc[n, rs] += jnp.dot(
+                dec_all[q, rs, :], enc_all[n, pl.ds(pl.multiple_of(q * depth, 128), depth), :],
+                preferred_element_type=F32)
+
+    def products(low, high):
+        pl.loop(0, 4 * levels)(lambda u: product_unit(u, low, high))
+
+    def pair_wait(low, high):
+        for lv in range(levels):
+            for h in range(2):
+                gap = jnp.maximum(lv - z, z - lv)
+                hop = jnp.where(gap == 0, 0, 2 * gap - 1 + h)
+
+                @pl.when(jnp.logical_and(hop >= low, hop <= high))
+                def _():
+                    pair_copy(lv, h, 1 - core).wait_recv()
 
     acc[...] = jnp.zeros_like(acc)
 
@@ -201,15 +215,8 @@
             for r in range(2):
                 for i in range(2, 4):
                     dec_copy(r, i, ring_from[r]).wait_recv()
-            for lv in range(levels):
-                @pl.when(jnp.logical_not(far(lv)))
-                def _():
-                    for h2 in range(2):
-                        pair_copy(lv, h2, 1 - core).wait_recv()
-
-            @pl.loop(0, 2)
-            def _(s):
-                quarter(jnp.where(s == 0, order[0], order[1]))
+            pair_wait(0, 4)
+            products(0, 4)
         if k == 2 * (levels - 2) + 1:
             for r in range(2):
                 del_copy(r, 1, ring_from[r]).wait_recv()
@@ -221,26 +228,28 @@
                     for b in range(rows // BLOCK):
                         value = jnp.zeros((win, BLOCK), masked.dtype)
                         for s in range(uact):
-                            on = flag(upb[d * wins + w, s], b, masked.dtype)
+                            on = flag(upb[s, d * wins + w], b, masked.dtype)
                             value = value + del_all[d, w, :, s * BLOCK:(s + 1) * BLOCK] * on
                         t = (d * wins + w) * win
                         masked[t:t + win, b * BLOCK:(b + 1) * BLOCK] = value
             prod[...] = lax.dot_general(
                 masked[...], grad_all[...], (((0,), (0,)), ((), ())), preferred_element_type=F32)
 
+            for r in range(2):
+                dec_copy(r, 4, diag).wait_recv()
+            pair_wait(5, 5)
+            products(5, 5)
+
     for r in range(2):
-        for i in range(4, 6):
-            dec_copy(r, i, diag).wait_recv()
-    for lv in range(levels):
-        @pl.when(far(lv))
-        def _():
-            for h2 in range(2):
-                pair_copy(lv, h2, 1 - core).wait_recv()
-
-    @pl.loop(2, 4)
-    def _(s):
-        quarter(jnp.where(s == 2, order[2], order[3]))
-    out[...] = acc[...] * prod[...]
+        dec_copy(r, 5, diag).wait_recv()
+    pair_wait(6, 6)
+    products(6, 6)
+    stores = []
+    for s in range(dact):
+        side, at = divmod(s * BLOCK, half)
+        res[s] = acc[side, :, at:at + BLOCK] * prod[:, s * BLOCK:(s + 1) * BLOCK]
+        stores.append(pltpu.make_async_copy(res.at[s], out.at[s], out_sem.at[s]))
+        stores[-1].start()
 
     for r in range(2):
         for i in range(3):
@@ -257,16 +266,35 @@
         pair_grad(lv, core).wait_send()
         for h in range(2):
             pair_copy(lv, h, core).wait_send()
-
-
-def spread(downb, scored, out):
-    for c in range(out.shape[1] // BLOCK):
-        slot, on = 0, 0
-        for s in range(downb.shape[0]):
-            hit = (downb[s] == c).astype(jnp.int32)
-            slot, on = slot + s * hit, on + hit
-        value = scored[:, pl.ds(pl.multiple_of(slot * BLOCK, BLOCK), BLOCK)]
-        out[:, c * BLOCK:(c + 1) * BLOCK] = jnp.where(on > 0, value, 0.0)
+    for copy in stores:
+        copy.wait()
+
+
+def spread(downb, scored, out, blank, held, load_sem, out_sem, blank_sem):
+    loads = [pltpu.make_async_copy(scored.at[s], held.at[s], load_sem.at[s]) for s in range(downb.shape[0])]
+    for copy in loads:
+        copy.start()
+    blank[...] = jnp.zeros_like(blank)
+    blocks = out.shape[1] // BLOCK
+
+    def each_blank(act):
+        for c in range(blocks):
+            used = sum((downb[s] == c).astype(jnp.int32) for s in range(downb.shape[0]))
+
+            @pl.when(used == 0)
+            def _():
+                act(pltpu.make_async_copy(blank, out.at[:, c * BLOCK:(c + 1) * BLOCK], blank_sem.at[c]))
+
+    each_blank(lambda copy: copy.start())
+    stores = []
+    for s, copy in enumerate(loads):
+        copy.wait()
+        cols = pl.ds(pl.multiple_of(downb[s] * BLOCK, BLOCK), BLOCK)
+        stores.append(pltpu.make_async_copy(held.at[s], out.at[:, cols], out_sem.at[s]))
+        stores[-1].start()
+    each_blank(lambda copy: copy.wait())
+    for copy in stores:
+        copy.wait()
 
 
 def ring_local(n_up, n_down, win, deltas, gradients, up_blocks, down_blocks, decoder, encoder):
@@ -281,24 +309,25 @@
     kind = decoder.dtype
     dma = pltpu.SemaphoreType.DMA
     smem, anywhere = pl.BlockSpec(memory_space=pltpu.SMEM), pl.BlockSpec(memory_space=pl.ANY)
-    vmem = pl.BlockSpec(memory_space=pltpu.VMEM)
+    hbm = pl.BlockSpec(memory_space=pltpu.HBM)
     hops = 2 * (levels - 1)
     scored = pl.pallas_call(
         functools.partial(gather_scores, n_up, n_down),
-        out_shape=jax.ShapeDtypeStruct((rows, used), F32),
-        in_specs=[smem, smem, anywhere, anywhere, anywhere, anywhere],
-        out_specs=vmem,
+        out_shape=jax.ShapeDtypeStruct((dact, rows, BLOCK), F32),
+        in_specs=[smem, smem, hbm, hbm, hbm, hbm],
+        out_specs=anywhere,
         scratch_shapes=[
             pltpu.VMEM((n_down, rows, depth), kind),
             pltpu.VMEM((height, cols), kind),
-            pltpu.VMEM((n_up * height, used), kind),
+            pltpu.VMEM((2, n_up * height, used // 2), kind),
             pltpu.VMEM(deltas.shape, kind),
             pltpu.VMEM((n_down, wins, win, uact * BLOCK), kind),
             pltpu.VMEM((toks, cols), kind),
             pltpu.VMEM((n_up * toks, used), kind),
             pltpu.VMEM((tokens, rows), kind),
+            pltpu.VMEM((2, rows, used // 2), F32),
             pltpu.VMEM((rows, used), F32),
-            pltpu.VMEM((rows, used), F32),
+            pltpu.VMEM((dact, rows, BLOCK), F32),
             dma((4,)),
             dma((2, 6)), dma((2, 6)),
             dma((2, 3)), dma((2, 3)),
@@ -306,17 +335,22 @@
             dma((2, levels - 1)), dma((2, levels - 1)),
             dma((levels, 2)), dma((levels, 2)),
             dma((levels,)), dma((levels,)),
+            dma((dact,)),
         ],
-        compiler_params=pltpu.CompilerParams(collective_id=0, has_side_effects=True),
+        compiler_params=pltpu.CompilerParams(collective_id=0, has_side_effects=True, vmem_limit_bytes=LARGE),
         name="gather_scores",
-    )(up_blocks, down_blocks, deltas, gradients, decoder, encoder)
-    tile = rows // 4
+    )(up_blocks.T, down_blocks, deltas, gradients, decoder, encoder)
     return pl.pallas_call(
         spread,
-        grid=(rows // tile,),
         out_shape=jax.ShapeDtypeStruct((rows, cols), F32),
-        in_specs=[smem, pl.BlockSpec((tile, used), lambda i: (i, 0))],
-        out_specs=pl.BlockSpec((tile, cols), lambda i: (i, 0)),
+        in_specs=[smem, anywhere],
+        out_specs=anywhere,
+        scratch_shapes=[
+            pltpu.VMEM((rows, BLOCK), F32),
+            pltpu.VMEM((dact, rows, BLOCK), F32),
+            dma((dact,)), dma((dact,)), dma((cols // BLOCK,)),
+        ],
+        compiler_params=pltpu.CompilerParams(vmem_limit_bytes=SMALL),
         name="spread",
     )(down_blocks, scored)
 

time: 56.9 us -> 57.7 us (1.014)
  local copies, waits for them, and re-layouts: 1.34 us -> 5.55 us
  Pallas kernels: 55.3 us -> 51.9 us
    unnamed x1 -> x12, local copies, waits for them, and re-layouts: 1.34 us -> 5.55 us
    pallas_call x1, Pallas kernels: 51.6 us -> 49.8 us  [ring_local(): pl.pallas_call(functools.partial(gather_scores, n_up, n_down), out_shape=...]
    pallas_call x1, Pallas kernels: 3.71 us -> 2.08 us  [ring_local(): pl.pallas_call(spread, out_shape=jax.ShapeDtypeStruct((rows, cols), F32),...]
where the time goes in v2:
time: 57.7 us; the launch traced here: 57.4 us
  Pallas kernels  51.9 us (90%)
  local copies, waits for them, and re-layouts  5.55 us (10%)
    pallas_call x1, Pallas kernels, ring_local(): pl.pallas_call(functools.partial(gather_scores, n_up, n_down), out_shape=...  49.8 us
    unnamed x12, local copies, waits for them, and re-layouts  5.55 us
    pallas_call x1, Pallas kernels, ring_local(): pl.pallas_call(spread, out_shape=jax.ShapeDtypeStruct((rows, cols), F32),...  2.08 us

profile of v2, /device:TPU:1, one launch (start us, length us, event | category | flops | bytes accessed | tf_op | source)
XLA Modules:
  0.0 57.4 jit_solution(5450514925284684947)
XLA Ops:
  0.0 0.0 copy-start
  0.0 1.3 %copy-done = bf16[512,1152]{1,0:T(8,128)(2,1)S(1)} copy-done((bf16[512,1152]{1,0:T(8,128)(2,1)S(1)}, bf16[512,1152]{1,0:T(8,128)(2,1)}, u32[]{:S(2)}) %copy-start) | copy-done | bytes 1179672
  1.3 0.0 copy-start.1
  1.3 1.3 %copy-done.1 = bf16[576,1024]{1,0:T(8,128)(2,1)S(1)} copy-done((bf16[576,1024]{1,0:T(8,128)(2,1)S(1)}, bf16[576,1024]{1,0:T(8,128)(2,1)}, u32[]{:S(2)}) %copy-start.1) | copy-done | bytes 1179672
  2.5 0.0 copy-start.2
  2.5 0.8 %copy-done.2 = bf16[64,512]{1,0:T(8,128)(2,1)S(1)} copy-done((bf16[64,512]{1,0:T(8,128)(2,1)S(1)}, bf16[64,512]{1,0:T(8,128)(2,1)}, u32[]{:S(2)}) %copy-start.2) | copy-done | bytes 65560
  3.4 0.0 copy-start.3
  3.4 0.8 %copy-done.3 = bf16[32,1024]{1,0:T(8,128)(2,1)S(1)} copy-done((bf16[32,1024]{1,0:T(8,128)(2,1)S(1)}, bf16[32,1024]{1,0:T(8,128)(2,1)}, u32[]{:S(2)}) %copy-start.3) | copy-done | bytes 65560
  4.2 0.0 copy-start.4
  4.2 0.7 %copy-done.4 = s32[4]{0:T(128)S(1)} copy-done((s32[4]{0:T(128)S(1)}, s32[4]{0:T(128)}, u32[]{:S(2)}) %copy-start.4) | copy-done | bytes 40
  4.9 0.0 copy-start.5
  4.9 0.7 %copy-done.5 = s32[8,2]{0,1:T(2,128)S(1)} copy-done((s32[8,2]{0,1:T(2,128)S(1)}, s32[8,2]{0,1:T(2,128)}, u32[]{:S(2)}) %copy-start.5) | copy-done | bytes 88
  5.6 49.8 %gather_scores.1.scored = f32[4,512,128]{2,1,0:T(8,128)S(1)} custom-call(s32[2,8]{1,0:T(2,128)S(1)} %bitcast.1, s32[4]{0:T(128)S(1)} %copy-done.4, bf16[64,512]{1,0:T(8,128)(2,1)S(1)} %copy-done.2, bf16[32,1024]{1,0:T(8,128)(2,1)S(1)} %copy-done.3, bf16[512,1152]{1,0:T(8,128)(2,1)S(1)} %copy-done, bf16[576,1024]{1,0:T(8,128)(2,1)S(1)} %copy-done.1), custom_call_target="tpu_custom_call" | custom-call | tf_op jit(solution)/shard_map/gather_scores/pallas_call | solution.py:314
  55.4 2.1 %spread.1 = f32[512,1024]{1,0:T(8,128)} custom-call(s32[4]{0:T(128)S(1)} %copy-done.4, f32[4,512,128]{2,1,0:T(8,128)S(1)} %gather_scores.1.scored), custom_call_target="tpu_custom_call" | custom-call | tf_op jit(solution)/shard_map/spread/pallas_call | solution.py:343
Async XLA Ops:
  0.0 1.3 %copy-start = (bf16[512,1152]{1,0:T(8,128)(2,1)S(1)}, bf16[512,1152]{1,0:T(8,128)(2,1)}, u32[]{:S(2)}) copy-start(bf16[512,1152]{1,0:T(8,128)(2,1)} %dec.1) | copy-start | bytes 3538948
  1.3 1.3 %copy-start.1 = (bf16[576,1024]{1,0:T(8,128)(2,1)S(1)}, bf16[576,1024]{1,0:T(8,128)(2,1)}, u32[]{:S(2)}) copy-start(bf16[576,1024]{1,0:T(8,128)(2,1)} %enc.1) | copy-start | bytes 3538948
  2.5 0.8 %copy-start.2 = (bf16[64,512]{1,0:T(8,128)(2,1)S(1)}, bf16[64,512]{1,0:T(8,128)(2,1)}, u32[]{:S(2)}) copy-start(bf16[64,512]{1,0:T(8,128)(2,1)} %deltas.1) | copy-start | bytes 196612
  3.4 0.8 %copy-start.3 = (bf16[32,1024]{1,0:T(8,128)(2,1)S(1)}, bf16[32,1024]{1,0:T(8,128)(2,1)}, u32[]{:S(2)}) copy-start(bf16[32,1024]{1,0:T(8,128)(2,1)} %grads.1) | copy-start | bytes 196612
  4.2 0.7 %copy-start.4 = (s32[4]{0:T(128)S(1)}, s32[4]{0:T(128)}, u32[]{:S(2)}) copy-start(s32[4]{0:T(128)} %downb.3) | copy-start | bytes 52
  4.9 0.7 %copy-start.5 = (s32[8,2]{0,1:T(2,128)S(1)}, s32[8,2]{0,1:T(2,128)}, u32[]{:S(2)}) copy-start(s32[8,2]{0,1:T(2,128)} %param.8) | copy-start | bytes 196

commit v3 on v2

--- a/solution.py
+++ b/solution.py
@@ -339,7 +339,7 @@
         ],
         compiler_params=pltpu.CompilerParams(collective_id=0, has_side_effects=True, vmem_limit_bytes=LARGE),
         name="gather_scores",
-    )(up_blocks.T, down_blocks, deltas, gradients, decoder, encoder)
+    )(*[pltpu.with_memory_space_constraint(x, pltpu.HBM) for x in (up_blocks.T, down_blocks, deltas, gradients, decoder, encoder)])
     return pl.pallas_call(
         spread,
         out_shape=jax.ShapeDtypeStruct((rows, cols), F32),
@@ -352,7 +352,7 @@
         ],
         compiler_params=pltpu.CompilerParams(vmem_limit_bytes=SMALL),
         name="spread",
-    )(down_blocks, scored)
+    )(pltpu.with_memory_space_constraint(down_blocks, pltpu.HBM), scored)
 
 
 def plain_local(deltas, gradients, up_blocks, down_blocks, decoder, encoder):

time: 57.7 us -> 52.6 us (0.912)
  local copies, waits for them, and re-layouts: 5.55 us -> 0 us
    unnamed x12 -> x0, local copies, waits for them, and re-layouts: 5.55 us -> none
where the time goes in v3:
time: 52.6 us; the launch traced here: 52.4 us
  Pallas kernels  52.4 us (100%)
    pallas_call x1, Pallas kernels, ring_local(): pl.pallas_call(functools.partial(gather_scores, n_up, n_down), out_shape=...  50.2 us
    pallas_call x1, Pallas kernels, ring_local(): pl.pallas_call(spread, out_shape=jax.ShapeDtypeStruct((rows, cols), F32),...  2.2 us

profile of v3, /device:TPU:1, one launch (start us, length us, event | category | flops | bytes accessed | tf_op | source)
XLA Modules:
  0.0 52.4 jit_solution(8075209616088913476)
XLA Ops:
  0.0 50.2 %gather_scores.1.scored = f32[4,512,128]{2,1,0:T(8,128)S(1)} custom-call(s32[2,8]{1,0:T(2,128)} %bitcast.1, s32[4]{0:T(128)} %downb.3, bf16[64,512]{1,0:T(8,128)(2,1)} %deltas.1, bf16[32,1024]{1,0:T(8,128)(2,1)} %grads.1, bf16[512,1152]{1,0:T(8,128)(2,1)} %dec.1, bf16[576,1024]{1,0:T(8,128)(2,1)} %enc.1), custom_call_target="tpu_custom_call" | custom-call | tf_op jit(solution)/shard_map/gather_scores/pallas_call | solution.py:314
  50.2 2.2 %spread.1 = f32[512,1024]{1,0:T(8,128)} custom-call(s32[4]{0:T(128)} %downb.3, f32[4,512,128]{2,1,0:T(8,128)S(1)} %gather_scores.1.scored), custom_call_target="tpu_custom_call" | custom-call | tf_op jit(solution)/shard_map/spread/pallas_call | solution.py:343
